TPU v7x, 32 devices: a whole 2x2x4 slice. The times are simulated.
32 devices in a mesh: pair: 16 (over z, y, x), sector: 2 (over core).
Axes of the slice: x: 2, y: 2, z: 4, core: 2. Of those that a mesh axis runs over, the one named last changes fastest.
Arguments:
- wavefunction: float32 [2, 512, 512], P('sector', 'pair'), may hold values from -6 to 6
- preconditioner: float32 [2, 512, 512], P('sector', 'pair'), may hold values from 0.5 to 4
- left_ops: float32 [48, 2, 512, 512], P('pair', 'sector'), may hold values from -0.25 to 0.25
- right_ops: float32 [48, 2, 512, 512], P('pair', 'sector'), may hold values from -0.02734375 to 0.02734375
- charges: int32 [48], P('pair'), may hold values from 0 to 2
- coupling: int32 [2, 3], P('sector'), may hold values 0 or 1
Outputs:
- new_state: float32 [2, 512, 512], P('sector', 'pair')
- new_image: float32 [2, 512, 512], P('sector', 'pair')
- energies: float32 [2], replicated
All inputs are finite; a program needn't handle non-finite values. No bound on the sum of `coupling` on one device may be relied on, other than what follows from the above.
Results may differ from a plain program's by a relative error of at most 0.0003.
Values sent between devices are 32-bit elements; how exact they have to be, the bound alone decides.
No kernel may reach another device: no remote copies, remote signals or barrier semaphores. Data moves between devices by JAX's collectives and lax.ppermute only.
A program may use at most 64 MiB of HBM per device.

v0:
```python
import math
import jax
import jax.numpy as jnp
from jax import lax
from jax.sharding import PartitionSpec as P

highest = lax.Precision.HIGHEST


def shifted(block, axis, distance):
    devices = range(lax.axis_size(axis))
    route = [((i - distance) % len(devices), i) for i in devices]
    return lax.ppermute(block, axis, route)


def product(first, second):
    return jnp.dot(first, second, precision=highest, preferred_element_type=jnp.float32)


def sigma_apply(vector, left_ops, right_ops, charges, coupling):
    lower_rows = shifted(vector, "sector", 1)
    upper_rows = shifted(vector, "sector", -1)
    gathered = (
        lax.all_gather(lower_rows, "pair", axis=1, tiled=True),
        lax.all_gather(vector, "pair", axis=1, tiled=True),
        lax.all_gather(upper_rows, "pair", axis=1, tiled=True),
    )
    stacked = jnp.concatenate(gathered, axis=0)
    own_block = stacked[1]
    targets = jnp.zeros_like(stacked)
    for which_pair in range(left_ops.shape[0]):
        left_block = left_ops[which_pair, 0]
        right_block = right_ops[which_pair, 0]
        charge_slot = charges[which_pair]
        allowed = lax.dynamic_index_in_dim(coupling[0], charge_slot, 0, keepdims=False).astype(
            jnp.float32
        )
        source_block = lax.dynamic_index_in_dim(stacked, charge_slot, 0, keepdims=False)
        forward = product(product(left_block, own_block), right_block.T)
        backward = product(product(left_block.T, source_block), right_block)
        current = lax.dynamic_index_in_dim(targets, charge_slot, 0, keepdims=False)
        targets = lax.dynamic_update_index_in_dim(
            targets, current + allowed * forward, charge_slot, 0
        )
        targets = targets.at[1].add(allowed * backward)
    from_below = shifted(targets[2], "sector", 1)
    from_above = shifted(targets[0], "sector", -1)
    combined = targets[1] + from_below + from_above
    return lax.psum_scatter(combined[None], "pair", scatter_dimension=1, tiled=True)


def per_device(wavefunction, preconditioner, left_ops, right_ops, charges, coupling):
    first_image = sigma_apply(wavefunction, left_ops, right_ops, charges, coupling)
    norm_sq, correlation = lax.psum(
        (jnp.sum(wavefunction * wavefunction), jnp.sum(wavefunction * first_image)),
        ("pair", "sector"),
    )
    theta = correlation / norm_sq
    inverse = lax.rsqrt(norm_sq)
    vector = wavefunction * inverse
    image = first_image * inverse
    residual = image - theta * vector
    correction = residual / preconditioner
    along, squared = lax.psum(
        (jnp.sum(vector * correction), jnp.sum(correction * correction)), ("pair", "sector")
    )
    orthogonal = correction - along * vector
    length_sq = squared - along * along
    basis = orthogonal * lax.rsqrt(length_sq + 1e-30)
    second_image = sigma_apply(basis, left_ops, right_ops, charges, coupling)
    corner, cross = lax.psum(
        (jnp.sum(basis * second_image), jnp.sum(vector * second_image)), ("pair", "sector")
    )
    half = (theta - corner) / 2.0
    lowest = (theta + corner) / 2.0 - jnp.sqrt(half * half + cross * cross)
    first_weight = corner - lowest
    second_weight = -cross
    size_norm = jnp.sqrt(first_weight * first_weight + second_weight * second_weight + 1e-30)
    entries = (
        lax.axis_size("sector")
        * lax.axis_size("pair")
        * wavefunction.shape[1]
        * wavefunction.shape[2]
    )
    scale = jnp.float32(math.sqrt(entries))
    factor_one = scale * first_weight / size_norm
    factor_two = scale * second_weight / size_norm
    new_state = factor_one * vector + factor_two * basis
    new_image = factor_one * image + factor_two * second_image
    energies = jnp.stack([theta, lowest])
    return (new_state, new_image, energies)


def solution(mesh):
    in_specs = (
        P("sector", "pair", None),
        P("sector", "pair", None),
        P("pair", "sector", None, None),
        P("pair", "sector", None, None),
        P("pair"),
        P("sector", None),
    )
    out_specs = (P("sector", "pair", None), P("sector", "pair", None), P())
    return jax.shard_map(
        per_device, mesh=mesh, in_specs=in_specs, out_specs=out_specs, check_vma=False
    )
```

profile of v0, /device:TPU:12, one launch (start us, length us, event | category | flops | bytes accessed | tf_op | source)
XLA Modules:
  0.0 604.5 jit_solution(9496863320256029471)
XLA Ops:
  21.0 45.0 %all-gather.5.cloned.1.call-done = f32[1,512,512]{2,1,0:T(8,128)} async-done(((f32[1,32,512]{2,1,0:T(8,128)}), f32[1,512,512]{2,1,0:T(8,128)}) %all-gather.5.cloned.1.call-update) | async-done | bytes 1048592 | tf_op jit(solution)/shard_map/all_gather | solution.py:25
  66.0 3.4 fusion.82
  69.4 2.0 broadcast.76.clone
  71.5 4.4 fusion.21
  75.9 2.8 fusion.72
  78.7 2.9 fusion.61
  81.5 41.8 %all-gather.7.cloned.1.call-done = f32[1,512,512]{2,1,0:T(8,128)} async-done(((f32[1,32,512]{2,1,0:T(8,128)}), f32[1,512,512]{2,1,0:T(8,128)}) %all-gather.7.cloned.1.call-update) | async-done | bytes 1048592 | tf_op jit(solution)/shard_map/all_gather | solution.py:24
  126.1 1.9 fusion.63
  128.0 1.9 fusion.74
  130.0 4.5 fusion.23
  135.8 2.8 fusion.18
  138.6 4.2 fusion.25
  144.1 2.9 fusion.14
  152.9 4.3 fusion.39
  157.2 68.8 %reduce-scatter.3.cloned.1.call-done = f32[1,32,512]{2,1,0:T(8,128)} async-done(((f32[1,512,512]{2,1,0:T(8,128)}), f32[1,32,512]{2,1,0:T(8,128)}) %reduce-scatter.3.cloned.1.call-update) | async-done | bytes 65552 | tf_op jit(solution)/shard_map/reduce_scatter | solution.py:49
  227.5 49.3 %all-reduce.2 = (f32[]{:T(128)}, f32[]{:T(128)}) all-reduce(f32[]{:T(128)} %get-tuple-element.80, f32[]{:T(128)} %get-tuple-element.79), channel_id=1, replica_groups=mesh['pair'=16,'sector'=2] {'pair','sector'}, use_global_device_ids=true, to_apply=%region_4.5 | all-reduce | flops 2 | bytes 16 | tf_op jit(solution)/shard_map/psum | solution.py:54
  280.4 38.5 %all-reduce.1 = (f32[]{:T(128)}, f32[]{:T(128)}) all-reduce(f32[]{:T(128)} %get-tuple-element.78, f32[]{:T(128)} %get-tuple-element.77), channel_id=1, replica_groups=mesh['pair'=16,'sector'=2] {'pair','sector'}, use_global_device_ids=true, to_apply=%region_8.9 | all-reduce | flops 2 | bytes 16 | tf_op jit(solution)/shard_map/psum | solution.py:64
  324.6 52.9 %all-gather.9.cloned.1.call-done = f32[1,512,512]{2,1,0:T(8,128)} async-done(((f32[1,32,512]{2,1,0:T(8,128)}), f32[1,512,512]{2,1,0:T(8,128)}) %all-gather.9.cloned.1.call-update) | async-done | bytes 1048592 | tf_op jit(solution)/shard_map/all_gather | solution.py:25
  377.5 4.7 fusion.50
  382.2 2.0 broadcast.76
  384.2 5.7 fusion.10
  389.9 4.5 fusion.48
  394.4 4.7 fusion.46
  399.0 35.6 %all-gather.11.cloned.1.call-done = f32[1,512,512]{2,1,0:T(8,128)} async-done(((f32[1,32,512]{2,1,0:T(8,128)}), f32[1,512,512]{2,1,0:T(8,128)}) %all-gather.11.cloned.1.call-update) | async-done | bytes 1048592 | tf_op jit(solution)/shard_map/all_gather | solution.py:24
  437.4 1.9 fusion.42
  441.3 4.2 fusion.29
  446.7 4.5 fusion.7
  451.2 4.4 fusion.31
  456.9 4.5 fusion.3
  467.4 4.3 fusion.36
  471.7 68.7 %reduce-scatter.5.cloned.1.call-done = f32[1,32,512]{2,1,0:T(8,128)} async-done(((f32[1,512,512]{2,1,0:T(8,128)}), f32[1,32,512]{2,1,0:T(8,128)}) %reduce-scatter.5.cloned.1.call-update) | async-done | bytes 65552 | tf_op jit(solution)/shard_map/reduce_scatter | solution.py:49
  541.9 49.2 %all-reduce = (f32[]{:T(128)}, f32[]{:T(128)}) all-reduce(f32[]{:T(128)} %get-tuple-element.76, f32[]{:T(128)} %get-tuple-element.75), channel_id=1, replica_groups=mesh['pair'=16,'sector'=2] {'pair','sector'}, use_global_device_ids=true, to_apply=%region_13.14 | all-reduce | flops 2 | bytes 16 | tf_op jit(solution)/shard_map/psum | solution.py:71
  (81 shorter events, 40.6 us)
Async XLA Ops:
  7.2 58.8 %all-gather.5.cloned.1.call-start = ((), (), s32[]{:S(2)}) async-start(), calls=%async_computation.2 | async-start | bytes 1114112 | tf_op jit(solution)/shard_map/all_gather | solution.py:25
  7.9 115.4 %all-gather.7.cloned.1.call-start = ((), (), s32[]{:S(2)}) async-start(), calls=%async_computation.3 | async-start | bytes 1114112 | tf_op jit(solution)/shard_map/all_gather | solution.py:24
  7.9 1.5 collective-permute-start
  9.5 0.6 copy-start.14
  10.1 215.9 %reduce-scatter.3.cloned.1.call-start = ((), (), s32[]{:S(2)}) async-start(), calls=%async_computation.4 | async-start | bytes 1114112 | tf_op jit(solution)/shard_map/reduce_scatter | solution.py:49
  69.4 6.5 %copy-start = (f32[3,1,512,512]{3,2,1,0:T(8,128)S(1)}, f32[3,1,512,512]{3,2,1,0:T(8,128)}, u32[]{:S(2)}) copy-start(f32[3,1,512,512]{3,2,1,0:T(8,128)} %param.20) | copy-start | bytes 9437188
  69.4 6.5 %copy-start.3 = (f32[1,512,512]{2,1,0:T(8,128)S(1)}, f32[1,512,512]{2,1,0:T(8,128)}, u32[]{:S(2)}) copy-start(f32[1,512,512]{2,1,0:T(8,128)} %all-gather.5.cloned.1.call-done) | copy-start | bytes 3145732
  123.3 2.7 copy-start.9
  126.1 3.9 copy-start.1
  130.0 5.8 copy-start.8
  138.6 5.5 copy-start.6
  148.7 2.7 collective-permute-start.1
  148.8 4.1 collective-permute-start.2
  151.2 74.9 %copy-start.11 = (f32[1,32,512]{2,1,0:T(8,128)S(1)}, f32[1,32,512]{2,1,0:T(8,128)}, u32[]{:S(2)}) copy-start(f32[1,32,512]{2,1,0:T(8,128)} %param.18) | copy-start | bytes 196612
  151.2 127.7 %copy-start.16 = (f32[1,32,512]{2,1,0:T(8,128)S(1)}, f32[1,32,512]{2,1,0:T(8,128)}, u32[]{:S(2)}) copy-start(f32[1,32,512]{2,1,0:T(8,128)} %param.19) | copy-start | bytes 196612
  157.2 220.3 %all-gather.9.cloned.1.call-start = ((), (), s32[]{:S(2)}) async-start(), calls=%async_computation.5 | async-start | bytes 1114112 | tf_op jit(solution)/shard_map/all_gather | solution.py:25
  322.1 112.5 %all-gather.11.cloned.1.call-start = ((), (), s32[]{:S(2)}) async-start(), calls=%async_computation.6 | async-start | bytes 1114112 | tf_op jit(solution)/shard_map/all_gather | solution.py:24
  322.2 1.5 collective-permute-start.3
  323.7 0.6 copy-start.15
  324.4 216.0 %reduce-scatter.5.cloned.1.call-start = ((), (), s32[]{:S(2)}) async-start(), calls=%async_computation.7 | async-start | bytes 1114112 | tf_op jit(solution)/shard_map/reduce_scatter | solution.py:49
  382.2 7.7 %copy-start.4 = (f32[1,512,512]{2,1,0:T(8,128)S(1)}, f32[1,512,512]{2,1,0:T(8,128)}, u32[]{:S(2)}) copy-start(f32[1,512,512]{2,1,0:T(8,128)} %all-gather.9.cloned.1.call-done) | copy-start | bytes 3145732
  434.6 2.7 copy-start.10
  437.4 3.9 copy-start.2
  441.3 5.5 copy-start.7
  451.2 5.7 copy-start.5
  463.1 2.7 collective-permute-start.4
  463.2 4.1 collective-permute-start.5
  465.6 74.7 %copy-start.12 = (f32[1,32,512]{2,1,0:T(8,128)S(1)}, f32[1,32,512]{2,1,0:T(8,128)}, u32[]{:S(2)}) copy-start(f32[1,32,512]{2,1,0:T(8,128)} %subtract_multiply_fusion) | copy-start | bytes 196612
  465.7 130.1 %copy-start.13 = (f32[1,32,512]{2,1,0:T(8,128)S(1)}, f32[1,32,512]{2,1,0:T(8,128)}, u32[]{:S(2)}) copy-start(f32[1,32,512]{2,1,0:T(8,128)} %reduce-scatter.3.cloned.1.call-done) | copy-start | bytes 196612
Sparse Core Ops, SparseCore 0:
  10.7 55.2 all-gather.4
  69.3 53.9 all-gather.6
  157.3 68.7 reduce-scatter.2
  322.3 55.1 all-gather.8
  380.6 53.9 all-gather.10
  471.8 68.5 reduce-scatter.4
where the time goes:
time: 615 us; the launch traced here: 605 us
  waiting for transfers between devices  320 us (52%)
  blocking collectives  137 us (22%)
  matrix products  84.9 us (14%)
  between operations  30.9 us (5%)
  local copies, waits for them, and re-layouts  22.4 us (4%)
  other arithmetic  7.79 us (1%)
    reduce_scatter x2, waiting for transfers between devices, sigma_apply(): lax.psum_scatter(combined[None], 'pair', scatter_dimension=1, tiled=True)  138 us
    all_gather x2, waiting for transfers between devices, sigma_apply(): lax.all_gather(vector, 'pair', axis=1, tiled=True)  97.9 us
    dot_general x24, matrix products, product(): jnp.dot(first, second, precision=highest, preferred_element_type=jnp.floa...  84.9 us
    all_gather x2, waiting for transfers between devices, sigma_apply(): lax.all_gather(lower_rows, 'pair', axis=1, tiled=True)  77.3 us
    psum x1, blocking collectives, per_device(): lax.psum((jnp.sum(wavefunction * wavefunction), jnp.sum(wavefunction * fi...  49.3 us
    psum x1, blocking collectives, per_device(): lax.psum((jnp.sum(basis * second_image), jnp.sum(vector * second_image)),...  49.2 us
    psum x1, blocking collectives, per_device(): lax.psum((jnp.sum(vector * correction), jnp.sum(correction * correction))...  38.5 us
  transfers between devices with their start and end apart: 12, of which 12 were waited for; matrix products, arithmetic and copies ran while one was open for 7% of the time, Pallas kernels for 0%

commit v1 on v0

--- a/solution.py
+++ b/solution.py
@@ -5,6 +5,27 @@
 from jax.sharding import PartitionSpec as P
 
 highest = lax.Precision.HIGHEST
+
+
+def joined_along(pieces, dim):
+    shape = list(pieces.shape[1:])
+    shape[dim] *= pieces.shape[0]
+    return jnp.moveaxis(pieces, 0, dim).reshape(shape)
+
+
+def doubled(x, axis):
+    length, index = (lax.axis_size(axis), lax.axis_index(axis))
+    blocks, stride = (x[None], 1)
+    while stride < length:
+        other = lax.ppermute(blocks, axis, [(i, i ^ stride) for i in range(length)])
+        low = index & stride == 0
+        blocks = jnp.concatenate([jnp.where(low, blocks, other), jnp.where(low, other, blocks)])
+        stride *= 2
+    return blocks
+
+
+def collect(x, axis, dim):
+    return joined_along(doubled(x, axis), dim)
 
 
 def shifted(block, axis, distance):
@@ -21,7 +42,7 @@
     lower_rows = shifted(vector, "sector", 1)
     upper_rows = shifted(vector, "sector", -1)
     gathered = (
-        lax.all_gather(lower_rows, "pair", axis=1, tiled=True),
+        collect(lower_rows, "pair", 1),
         lax.all_gather(vector, "pair", axis=1, tiled=True),
         lax.all_gather(upper_rows, "pair", axis=1, tiled=True),
     )

time: 615 us -> 647 us (1.052)
  other arithmetic: 7.79 us -> 19.6 us
  starting transfers between devices: 1.69 us -> 13.2 us
  matrix products: 84.9 us -> 94.3 us
  local copies, waits for them, and re-layouts: 22.4 us -> 15.5 us
    ppermute x0 -> x8, waiting for transfers between devices: none -> 60.2 us  [doubled(): other = lax.ppermute(blocks, axis, [(i, i ^ stride) for i in range(length)])]
    all_gather x2, waiting for transfers between devices: 97.9 us -> 43.9 us  [sigma_apply(): lax.all_gather(vector, 'pair', axis=1, tiled=True)]
    ppermute x0 -> x8, starting transfers between devices: none -> 11.7 us  [doubled(): other = lax.ppermute(blocks, axis, [(i, i ^ stride) for i in range(length)])]
    dot_general x24, matrix products: 84.9 us -> 94.3 us  [product(): jnp.dot(first, second, precision=highest, preferred_element_type=jnp.floa...]
    concatenate x0 -> x10, other arithmetic: none -> 8.21 us  [the longest x2 4.32 us: sigma_apply(): stacked = jnp.concatenate(gathered, axis=0)]
  transfers between devices with their start and end apart: 12 -> 20, of which waited for: 12 -> 20; matrix products, arithmetic and copies ran while one was open for 7% -> 8% of each run, Pallas kernels for 0% -> 0%
where the time goes in v1:
time: 647 us; the launch traced here: 637 us
  waiting for transfers between devices  326 us (50%)
  blocking collectives  137 us (21%)
  matrix products  94.3 us (15%)
  between operations  31 us (5%)
  other arithmetic  19.6 us (3%)
  local copies, waits for them, and re-layouts  15.5 us (2%)
  starting transfers between devices  13.2 us (2%)
    reduce_scatter x2, waiting for transfers between devices, sigma_apply(): lax.psum_scatter(combined[None], 'pair', scatter_dimension=1, tiled=True)  137 us
    dot_general x24, matrix products, product(): jnp.dot(first, second, precision=highest, preferred_element_type=jnp.floa...  94.3 us
    all_gather x2, waiting for transfers between devices, sigma_apply(): lax.all_gather(upper_rows, 'pair', axis=1, tiled=True)  77.8 us
    ppermute x8, waiting for transfers between devices, doubled(): other = lax.ppermute(blocks, axis, [(i, i ^ stride) for i in range(length)])  60.2 us
    psum x1, blocking collectives, per_device(): lax.psum((jnp.sum(wavefunction * wavefunction), jnp.sum(wavefunction * fi...  49.3 us
    psum x1, blocking collectives, per_device(): lax.psum((jnp.sum(basis * second_image), jnp.sum(vector * second_image)),...  49.2 us
    all_gather x2, waiting for transfers between devices, sigma_apply(): lax.all_gather(vector, 'pair', axis=1, tiled=True)  43.9 us
    psum x1, blocking collectives, per_device(): lax.psum((jnp.sum(vector * correction), jnp.sum(correction * correction))...  38.5 us
  transfers between devices with their start and end apart: 20, of which 20 were waited for; matrix products, arithmetic and copies ran while one was open for 8% of the time, Pallas kernels for 0%

profile of v1, /device:TPU:12, one launch (start us, length us, event | category | flops | bytes accessed | tf_op | source)
XLA Modules:
  0.0 637.0 jit_solution(17018722894604995330)
XLA Ops:
  14.4 4.5 collective-permute-done.2
  19.5 6.3 collective-permute-done.3
  40.2 11.7 %collective-permute-done.4 = f32[8,1,32,512]{3,2,1,0:T(8,128)} collective-permute-done((f32[8,1,32,512]{3,2,1,0:T(8,128)}, f32[8,1,32,512]{3,2,1,0:T(8,128)}, u32[]{:S(2)}, u32[]{:S(2)}) %collective-permute-start.4) | collective-permute-done | bytes 524320 | tf_op jit(solution)/shard_map/ppermute | solution.py:20
  54.2 25.0 %all-gather.5.cloned.1.call-done = f32[1,512,512]{2,1,0:T(8,128)} async-done(((f32[1,32,512]{2,1,0:T(8,128)}), f32[1,512,512]{2,1,0:T(8,128)}) %all-gather.5.cloned.1.call-update) | async-done | bytes 1048592 | tf_op jit(solution)/shard_map/all_gather | solution.py:46
  79.2 3.1 fusion.82
  84.3 4.0 fusion.21
  88.4 2.9 fusion.72
  94.1 42.4 %all-gather.7.cloned.1.call-done = f32[1,512,512]{2,1,0:T(8,128)} async-done(((f32[1,32,512]{2,1,0:T(8,128)}), f32[1,512,512]{2,1,0:T(8,128)}) %all-gather.7.cloned.1.call-update) | async-done | bytes 1048592 | tf_op jit(solution)/shard_map/all_gather | solution.py:47
  142.8 4.1 fusion.23
  148.2 2.9 fusion.18
  151.1 4.2 fusion.25
  156.5 2.9 fusion.14
  165.3 14.5 %fusion.39 = f32[1,512,512]{2,1,0:T(8,128)} fusion(f32[512,512]{1,0:T(8,128)S(1)} %collective-permute-done.6, f32[512,512]{1,0:T(8,128)S(1)} %collective-permute-done.5, f32[512,512]{1,0:T(8,128)S(1)} %fusion.52, f32[3,512,512]{2,1,0:T(8,128)} %fusion.14, f32[3,1,512,512]{3,2,1,0:T(8,128)S(1)} %copy-done.1, f32[]{:T(128)} %bitcast.20), kind=kOutput, calls=%fused_computation.53 | convolution fusion | flops 1611661312 | bytes 6291460 | tf_op jit(solution)/shard_map/dot_general | solution.py:38
  179.9 68.7 %reduce-scatter.3.cloned.1.call-done = f32[1,32,512]{2,1,0:T(8,128)} async-done(((f32[1,512,512]{2,1,0:T(8,128)}), f32[1,32,512]{2,1,0:T(8,128)}) %reduce-scatter.3.cloned.1.call-update) | async-done | bytes 65552 | tf_op jit(solution)/shard_map/reduce_scatter | solution.py:70
  250.0 49.3 %all-reduce.2 = (f32[]{:T(128)}, f32[]{:T(128)}) all-reduce(f32[]{:T(128)} %get-tuple-element.80, f32[]{:T(128)} %get-tuple-element.79), channel_id=1, replica_groups=mesh['pair'=16,'sector'=2] {'pair','sector'}, use_global_device_ids=true, to_apply=%region_4.5 | all-reduce | flops 2 | bytes 16 | tf_op jit(solution)/shard_map/psum | solution.py:75
  302.9 38.5 %all-reduce.1 = (f32[]{:T(128)}, f32[]{:T(128)}) all-reduce(f32[]{:T(128)} %get-tuple-element.78, f32[]{:T(128)} %get-tuple-element.77), channel_id=1, replica_groups=mesh['pair'=16,'sector'=2] {'pair','sector'}, use_global_device_ids=true, to_apply=%region_8.9 | all-reduce | flops 2 | bytes 16 | tf_op jit(solution)/shard_map/psum | solution.py:85
  350.6 5.0 collective-permute-done.9
  358.2 5.0 collective-permute-done.10
  366.8 22.6 %collective-permute-done.11 = f32[8,1,32,512]{3,2,1,0:T(8,128)} collective-permute-done((f32[8,1,32,512]{3,2,1,0:T(8,128)}, f32[8,1,32,512]{3,2,1,0:T(8,128)}, u32[]{:S(2)}, u32[]{:S(2)}) %collective-permute-start.11) | collective-permute-done | bytes 524320 | tf_op jit(solution)/shard_map/ppermute | solution.py:20
  391.7 18.8 %all-gather.9.cloned.1.call-done = f32[1,512,512]{2,1,0:T(8,128)} async-done(((f32[1,32,512]{2,1,0:T(8,128)}), f32[1,512,512]{2,1,0:T(8,128)}) %all-gather.9.cloned.1.call-update) | async-done | bytes 1048592 | tf_op jit(solution)/shard_map/all_gather | solution.py:46
  410.6 4.7 fusion.50
  417.3 5.7 fusion.10
  423.0 4.5 fusion.48
  427.5 4.7 fusion.46
  432.2 35.5 %all-gather.11.cloned.1.call-done = f32[1,512,512]{2,1,0:T(8,128)} async-done(((f32[1,32,512]{2,1,0:T(8,128)}), f32[1,512,512]{2,1,0:T(8,128)}) %all-gather.11.cloned.1.call-update) | async-done | bytes 1048592 | tf_op jit(solution)/shard_map/all_gather | solution.py:47
  473.7 4.2 fusion.29
  479.2 4.5 fusion.7
  483.7 4.4 fusion.31
  489.4 4.5 fusion.3
  499.9 4.3 fusion.36
  504.2 68.7 %reduce-scatter.5.cloned.1.call-done = f32[1,32,512]{2,1,0:T(8,128)} async-done(((f32[1,512,512]{2,1,0:T(8,128)}), f32[1,32,512]{2,1,0:T(8,128)}) %reduce-scatter.5.cloned.1.call-update) | async-done | bytes 65552 | tf_op jit(solution)/shard_map/reduce_scatter | solution.py:70
  574.3 49.2 %all-reduce = (f32[]{:T(128)}, f32[]{:T(128)}) all-reduce(f32[]{:T(128)} %get-tuple-element.76, f32[]{:T(128)} %get-tuple-element.75), channel_id=1, replica_groups=mesh['pair'=16,'sector'=2] {'pair','sector'}, use_global_device_ids=true, to_apply=%region_13.14 | all-reduce | flops 2 | bytes 16 | tf_op jit(solution)/shard_map/psum | solution.py:92
  (115 shorter events, 75.0 us)
Async XLA Ops:
  7.2 24.0 %copy-start.18 = (s32[3]{0:T(128)S(1)}, s32[3]{0:T(128)}, u32[]{:S(2)}) copy-start(s32[3]{0:T(128)} %param.22) | copy-start | bytes 40
  7.2 30.4 %copy-start.19 = (s32[1,3]{1,0:T(1,128)S(1)}, s32[1,3]{1,0:T(1,128)}, u32[]{:S(2)}) copy-start(s32[1,3]{1,0:T(1,128)} %param.23) | copy-start | bytes 40
  7.2 72.0 %all-gather.5.cloned.1.call-start = ((), (), s32[]{:S(2)}) async-start(), calls=%async_computation.2 | async-start | bytes 1114112 | tf_op jit(solution)/shard_map/all_gather | solution.py:46
  7.9 128.6 %all-gather.7.cloned.1.call-start = ((), (), s32[]{:S(2)}) async-start(), calls=%async_computation.3 | async-start | bytes 1114112 | tf_op jit(solution)/shard_map/all_gather | solution.py:47
  8.0 1.5 collective-permute-start
  9.5 4.3 collective-permute-start.1
  13.8 5.0 collective-permute-start.2
  18.9 6.9 %collective-permute-start.3 = (f32[4,1,32,512]{3,2,1,0:T(8,128)S(1)}, f32[4,1,32,512]{3,2,1,0:T(8,128)}, u32[]{:S(2)}, u32[]{:S(2)}) collective-permute-start(f32[4,1,32,512]{3,2,1,0:T(8,128)S(1)} %pad_maximum_fusion.6), channel_id=1, source_target_pairs={{0,8},{2,10},{4,12},{6,14},{8,0},{10,2},{12,4},{14,6},{16,24},{18,... | collective-permute-start | bytes 786440 | tf_op jit(solution)/shard_map/ppermute | solution.py:20
  19.5 59.7 %copy-start = (f32[3,1,512,512]{3,2,1,0:T(8,128)S(1)}, f32[3,1,512,512]{3,2,1,0:T(8,128)}, u32[]{:S(2)}) copy-start(f32[3,1,512,512]{3,2,1,0:T(8,128)} %param.20) | copy-start | bytes 9437188
  28.4 23.5 %collective-permute-start.4 = (f32[8,1,32,512]{3,2,1,0:T(8,128)}, f32[8,1,32,512]{3,2,1,0:T(8,128)}, u32[]{:S(2)}, u32[]{:S(2)}) collective-permute-start(f32[8,1,32,512]{3,2,1,0:T(8,128)} %pad_maximum_fusion.4), channel_id=1, source_target_pairs={{0,16},{2,18},{4,20},{6,22},{8,24},{10,26},{12,28},{14,30},{16,0},... | collective-permute-start | bytes 1572872 | tf_op jit(solution)/shard_map/ppermute | solution.py:20
  31.1 217.5 %reduce-scatter.3.cloned.1.call-start = ((), (), s32[]{:S(2)}) async-start(), calls=%async_computation.4 | async-start | bytes 1114112 | tf_op jit(solution)/shard_map/reduce_scatter | solution.py:70
  82.3 6.1 copy-start.3
  142.5 5.7 copy-start.8
  161.1 2.7 collective-permute-start.5
  161.2 4.1 collective-permute-start.6
  163.6 85.0 %copy-start.9 = (f32[1,32,512]{2,1,0:T(8,128)S(1)}, f32[1,32,512]{2,1,0:T(8,128)}, u32[]{:S(2)}) copy-start(f32[1,32,512]{2,1,0:T(8,128)} %param.18) | copy-start | bytes 196612
  163.6 137.8 %copy-start.17 = (f32[1,32,512]{2,1,0:T(8,128)S(1)}, f32[1,32,512]{2,1,0:T(8,128)}, u32[]{:S(2)}) copy-start(f32[1,32,512]{2,1,0:T(8,128)} %param.19) | copy-start | bytes 196612
  179.8 230.7 %all-gather.9.cloned.1.call-start = ((), (), s32[]{:S(2)}) async-start(), calls=%async_computation.5 | async-start | bytes 1114112 | tf_op jit(solution)/shard_map/all_gather | solution.py:46
  344.6 123.1 %all-gather.11.cloned.1.call-start = ((), (), s32[]{:S(2)}) async-start(), calls=%async_computation.6 | async-start | bytes 1114112 | tf_op jit(solution)/shard_map/all_gather | solution.py:47
  344.7 1.5 collective-permute-start.7
  346.2 20.5 %copy-start.16 = (f32[1,32,512]{2,1,0:T(8,128)}, f32[1,32,512]{2,1,0:T(8,128)S(1)}, u32[]{:S(2)}) copy-start(f32[1,32,512]{2,1,0:T(8,128)S(1)} %collective-permute-done.7) | copy-start | bytes 196612
  346.2 4.3 collective-permute-start.8
  350.5 5.0 collective-permute-start.9
  355.6 7.6 %collective-permute-start.10 = (f32[4,1,32,512]{3,2,1,0:T(8,128)S(1)}, f32[4,1,32,512]{3,2,1,0:T(8,128)S(1)}, u32[]{:S(2)}, u32[]{:S(2)}) collective-permute-start(f32[4,1,32,512]{3,2,1,0:T(8,128)S(1)} %pad_maximum_fusion.7), channel_id=1, source_target_pairs={{0,8},{2,10},{4,12},{6,14},{8,0},{10,2},{12,4},{14,6},{16,24},{18,... | collective-permute-start | bytes 786440 | tf_op jit(solution)/shard_map/ppermute | solution.py:20
  364.8 24.6 %collective-permute-start.11 = (f32[8,1,32,512]{3,2,1,0:T(8,128)}, f32[8,1,32,512]{3,2,1,0:T(8,128)}, u32[]{:S(2)}, u32[]{:S(2)}) collective-permute-start(f32[8,1,32,512]{3,2,1,0:T(8,128)} %pad_maximum_fusion.5), channel_id=1, source_target_pairs={{0,16},{2,18},{4,20},{6,22},{8,24},{10,26},{12,28},{14,30},{16,0},... | collective-permute-start | bytes 1572872 | tf_op jit(solution)/shard_map/ppermute | solution.py:20
  366.8 206.1 %reduce-scatter.5.cloned.1.call-start = ((), (), s32[]{:S(2)}) async-start(), calls=%async_computation.7 | async-start | bytes 1114112 | tf_op jit(solution)/shard_map/reduce_scatter | solution.py:70
  415.3 7.7 %copy-start.4 = (f32[1,512,512]{2,1,0:T(8,128)S(1)}, f32[1,512,512]{2,1,0:T(8,128)}, u32[]{:S(2)}) copy-start(f32[1,512,512]{2,1,0:T(8,128)} %all-gather.9.cloned.1.call-done) | copy-start | bytes 3145732
  483.7 5.7 copy-start.5
  495.6 2.7 collective-permute-start.12
  495.7 4.1 collective-permute-start.13
  498.1 74.7 %copy-start.13 = (f32[1,32,512]{2,1,0:T(8,128)S(1)}, f32[1,32,512]{2,1,0:T(8,128)}, u32[]{:S(2)}) copy-start(f32[1,32,512]{2,1,0:T(8,128)} %subtract_multiply_fusion) | copy-start | bytes 196612
  498.2 130.0 %copy-start.14 = (f32[1,32,512]{2,1,0:T(8,128)S(1)}, f32[1,32,512]{2,1,0:T(8,128)}, u32[]{:S(2)}) copy-start(f32[1,32,512]{2,1,0:T(8,128)} %reduce-scatter.3.cloned.1.call-done) | copy-start | bytes 196612
  (8 other events, 25.6 us)
Sparse Core Ops, SparseCore 0:
  10.7 68.3 all-gather.4
  82.5 53.9 all-gather.6
  180.0 68.5 reduce-scatter.2
  344.8 65.7 all-gather.8
  413.7 53.9 all-gather.10
  504.3 68.5 reduce-scatter.4
